TPU v7x, 8 devices: a whole 2x2x1 slice. The times are simulated.
8 devices in a mesh: dp: 1 (over z), ep: 8 (over y, x, core).
Axes of the slice: x: 2, y: 2, z: 1, core: 2. Of those that a mesh axis runs over, the one named last changes fastest.
Arguments:
- tokens: bfloat16 [1024, 2048], P(('dp', 'ep'))
- expert_ids: int32 [1024, 8], P(('dp', 'ep'))
- norm_gain: bfloat16 [2048], replicated
- w_router: bfloat16 [2048, 64], replicated
- w_gate: bfloat16 [64, 2048, 1024], P('ep')
- w_up: bfloat16 [64, 2048, 1024], P('ep')
- w_down: bfloat16 [64, 1024, 2048], P('ep')
Outputs:
- output: bfloat16 [1024, 2048], P(('dp', 'ep'))
All inputs are finite; a program needn't handle non-finite values.
Results may differ from a plain program's by a relative error of at most 0.00578916.
Values are sent between devices in bfloat16 or wider.
A program may use at most 1 GiB of HBM per device.

v0:
```python
import jax
import jax.numpy as jnp
from jax import lax
from jax.sharding import PartitionSpec as P

NORM_EPS = 1e-5


def rms_norm(tok_rows, norm_gain):
    tok32 = tok_rows.astype(jnp.float32)
    inv_rms = lax.rsqrt(jnp.mean(tok32 * tok32, axis=1, keepdims=True) + NORM_EPS)
    return (tok32 * inv_rms * norm_gain.astype(jnp.float32)).astype(jnp.bfloat16)


def expert_ffn(rows, w_gate, w_up, w_down, group_sizes):
    hidden_gate = lax.ragged_dot(rows, w_gate, group_sizes, preferred_element_type=jnp.float32)
    hidden_up = lax.ragged_dot(rows, w_up, group_sizes, preferred_element_type=jnp.float32)
    swiglu_out = (jax.nn.silu(hidden_gate) * hidden_up).astype(jnp.bfloat16)
    return lax.ragged_dot(swiglu_out, w_down, group_sizes, preferred_element_type=jnp.float32).astype(jnp.bfloat16)


def route_plan(expert_ids, ep_size, e_local, send_max):
    tok_count, top_k = expert_ids.shape
    pairs = tok_count * top_k
    flat_ids = expert_ids.reshape(pairs)
    sort_order = jnp.argsort(flat_ids, stable=True)
    sorted_dev = flat_ids[sort_order] // e_local
    expert_count = jnp.bincount(flat_ids, length=ep_size * e_local).astype(jnp.int32)
    dev_count = expert_count.reshape(ep_size, e_local).sum(axis=1)
    dev_start = jnp.cumsum(dev_count) - dev_count
    slot_sorted = sorted_dev * send_max + jnp.arange(pairs) - dev_start[sorted_dev]
    slot_of_pair = jnp.zeros((pairs,), jnp.int32).at[sort_order].set(slot_sorted)
    sorted_pos = jnp.minimum(dev_start[:, None] + jnp.arange(send_max)[None, :], pairs - 1)
    send_tok = (sort_order[sorted_pos] // top_k).reshape(ep_size * send_max)
    return expert_count.reshape(ep_size, e_local), slot_of_pair, send_tok


def recv_plan(recv_count, send_max, recv_max):
    ep_size, e_local = recv_count.shape
    row_end = jnp.cumsum(recv_count, axis=1)
    row_begin = row_end - recv_count
    slot_rank = jnp.arange(send_max)
    slot_expert = jnp.sum(row_end[:, None, :] <= slot_rank[None, :, None], axis=2)
    expert_safe = jnp.minimum(slot_expert, e_local - 1)
    expert_total = recv_count.sum(axis=0)
    expert_start = jnp.cumsum(expert_total) - expert_total
    src_before = jnp.cumsum(recv_count, axis=0) - recv_count
    offset = expert_start[None, :] + src_before - row_begin
    compact_pos = jnp.where(slot_expert < e_local, jnp.take_along_axis(offset, expert_safe, axis=1) + slot_rank[None, :], recv_max).reshape(ep_size * send_max)
    compact_src = jnp.zeros((recv_max,), jnp.int32).at[compact_pos].set(jnp.arange(ep_size * send_max), mode='drop')
    return expert_total, compact_src, jnp.minimum(compact_pos, recv_max - 1)


def solution(mesh):
    ep_size = mesh.shape['ep']

    def device_step(tokens, expert_ids, norm_gain, w_router, w_gate, w_up, w_down):
        tok_count, top_k = expert_ids.shape
        width = tokens.shape[1]
        e_local = w_gate.shape[0]
        pairs = tok_count * top_k
        send_max = 2 * pairs // ep_size
        recv_max = 3 * pairs // 2
        normed = rms_norm(tokens, norm_gain)
        router_prob = jax.nn.softmax(jnp.dot(normed, w_router, preferred_element_type=jnp.float32), axis=1)
        gate_vals = jnp.take_along_axis(router_prob, expert_ids, axis=1)
        send_count, slot_of_pair, send_tok = route_plan(expert_ids, ep_size, e_local, send_max)
        send_rows = normed[send_tok].reshape(ep_size, send_max, width)
        recv_count = lax.all_to_all(send_count, 'ep', 0, 0, tiled=True)
        recv_rows = lax.all_to_all(send_rows, 'ep', 0, 0, tiled=True)
        expert_total, compact_src, back_pos = recv_plan(recv_count, send_max, recv_max)
        compact_rows = recv_rows.reshape(ep_size * send_max, width)[compact_src]
        expert_out = expert_ffn(compact_rows, w_gate, w_up, w_down, expert_total)
        back_rows = expert_out[back_pos].reshape(ep_size, send_max, width)
        home_rows = lax.all_to_all(back_rows, 'ep', 0, 0, tiled=True)
        pair_out = home_rows.reshape(ep_size * send_max, width)[slot_of_pair].reshape(tok_count, top_k, width)
        moe_sum = jnp.sum(gate_vals[:, :, None] * pair_out, axis=1)
        return (tokens.astype(jnp.float32) + moe_sum).astype(jnp.bfloat16)

    row_spec = P(('dp', 'ep'), None)
    expert_spec = P('ep', None, None)
    return jax.shard_map(device_step, mesh=mesh, in_specs=(row_spec, row_spec, P(None), P(None, None), expert_spec, expert_spec, expert_spec), out_specs=row_spec, check_vma=False)
```

profile of v0, /device:TPU:0, one launch (start us, length us, event | category | flops | bytes accessed | tf_op | source)
XLA Modules:
  0.0 394.4 jit_solution(17379483356102522816)
XLA Ops:
  0.0 0.8 broadcast_maximum_fusion
  1.0 7.6 %scatter_custom_fusion = s32[64]{0:T(128)S(1)} fusion(s32[1024]{0:T(1024)S(1)} %reshape.509, s32[1024]{0:T(1024)S(1)} %broadcast.445, s32[]{:T(128)} %constant.46.clone.1), kind=kCustom, calls=%fused_computation.90 | custom fusion | flops 1024 | bytes 260 | tf_op jit(solution)/shard_map/scatter-add | solution.py:28
  9.3 4.3 %all-to-all-start.1 = ((s32[8,1,8]{2,1,0:T(1,128)}), s32[8,1,8]{2,1,0:T(1,128)S(1)}, u32[]{:S(2)}, u32[]{:S(2)}) async-start(s32[8,1,8]{2,1,0:T(1,128)} %bitcast.1), calls=%async_computation.1 | async-start | bytes 8192 | tf_op jit(solution)/shard_map/all_to_all | solution.py:69
  13.6 0.8 copy.37
  14.4 1.2 fusion.1
  15.7 0.7 convert_element_type.29
  16.9 4.4 %sort.17 = (s32[1024]{0:T(1024)}, s32[1024]{0:T(1024)S(1)}) sort(s32[1024]{0:T(1024)S(1)} %reshape.421, s32[1024]{0:T(1024)S(1)} %iota.21), dimensions={0}, to_apply=%region_3.0 | sort | flops 10240 | bytes 16384 | tf_op jit(solution)/shard_map/jit(argsort)/sort | solution.py:26
  21.2 8.6 %gather_fusion = s32[2048]{0:T(1024)S(1)} fusion(s32[1024]{0:T(1024)S(1)} %get-tuple-element.6, s32[2048]{0:T(1024)S(1)} %broadcast_clamp_fusion.2), kind=kCustom, calls=%fused_computation | custom fusion | bytes 24576 | tf_op jit(solution)/shard_map/gather | solution.py:34
  30.1 11.0 %gather_fusion.1 = bf16[2048,2048]{1,0:T(8,128)(2,1)} fusion(bf16[128,2048]{1,0:T(8,128)(2,1)S(1)} %fusion.3, s32[2048]{0:T(1024)S(1)} %broadcast_clamp_fusion.1), kind=kCustom, calls=%fused_computation.1 | custom fusion | bytes 16785408 | tf_op jit(solution)/shard_map/gather | solution.py:68
  41.1 3.7 all-to-all-start
  45.6 1.5 ragged-dot-metadata
  47.1 0.8 reduce-window.16
  48.8 9.1 %gather_fusion.7 = s32[2048]{0:T(1024)S(1)} fusion(s32[8,8]{1,0:T(8,128)S(1)} %subtract_subtract_fusion, s32[2048]{0:T(1024)S(1)} %bitcast.63), kind=kCustom, calls=%fused_computation.7 | custom fusion | bytes 32768 | tf_op jit(solution)/shard_map/jit(take_along_axis)/gather | solution.py:49
  58.0 8.0 %scatter_custom_fusion.1 = s32[1536]{0:T(1024)S(1)} fusion(s32[2048]{0:T(1024)S(1)} %bitcast.79, s32[2048]{0:T(1024)S(1)} %iota.22, s32[]{:T(128)} %constant.46.clone.1), kind=kCustom, calls=%fused_computation.79 | custom fusion | bytes 6148 | tf_op jit(solution)/shard_map/scatter | solution.py:50
  66.1 72.7 %all-to-all-done = bf16[8,256,2048]{2,1,0:T(8,128)(2,1)} async-done(((bf16[8,256,2048]{2,1,0:T(8,128)(2,1)}), bf16[8,256,2048]{2,1,0:T(8,128)(2,1)}, u32[]{:S(2)}, u32[]{:S(2)}) %all-to-all-start) | async-done | bytes 8388640 | tf_op jit(solution)/shard_map/all_to_all | solution.py:70
  138.8 17.1 %gather_fusion.2 = bf16[1536,2048]{1,0:T(8,128)(2,1)} fusion(bf16[2048,2048]{1,0:T(8,128)(2,1)} %bitcast.7, s32[2048]{0:T(1024)S(1)} %pad_clamp_fusion), kind=kCustom, calls=%fused_computation.2 | custom fusion | bytes 12589056 | tf_op jit(solution)/shard_map/gather | solution.py:72
  156.0 24.6 %ragged-dot-none.2 = f32[1536,1024]{1,0:T(8,128)} custom-call(s32[1]{0:T(128)} %get-tuple-element.7, s32[9]{0:T(128)} %get-tuple-element.8, s32[13]{0:T(128)} %get-tuple-element.9, s32[13]{0:T(128)} %get-tuple-element.10, s32[1]{0:T(128)} %get-tuple-element.7, bf16[1536,2048]{1,0:T(8,128)(2,1)} %gather_fusion.2, bf16[8,2048,1024]{2,1,0:T(8,128)(2,1)} %param.11), custom_call_target="tpu_custom_call" | custom-call | flops 6442450944 | bytes 46137376 | tf_op jit(solution)/shard_map/ragged_dot_general/ragged-dot-none
  180.6 24.5 %ragged-dot-none.1 = f32[1536,1024]{1,0:T(8,128)} custom-call(s32[1]{0:T(128)} %get-tuple-element.7, s32[9]{0:T(128)} %get-tuple-element.8, s32[13]{0:T(128)} %get-tuple-element.9, s32[13]{0:T(128)} %get-tuple-element.10, s32[1]{0:T(128)} %get-tuple-element.7, bf16[1536,2048]{1,0:T(8,128)(2,1)} %gather_fusion.2, bf16[8,2048,1024]{2,1,0:T(8,128)(2,1)} %param.12), custom_call_target="tpu_custom_call" | custom-call | flops 6442450944 | bytes 46137376 | tf_op jit(solution)/shard_map/ragged_dot_general/ragged-dot-none
  205.1 6.8 %multiply_convert_fusion = bf16[1536,1024]{1,0:T(8,128)(2,1)} fusion(f32[1536,1024]{1,0:T(8,128)} %ragged-dot-none.1, f32[1536,1024]{1,0:T(8,128)} %ragged-dot-none.2), kind=kLoop, calls=%fused_computation.13 | loop fusion | flops 9437184 | bytes 15728640 | tf_op jit(solution)/shard_map/convert_element_type | solution.py:18
  211.9 25.8 %ragged-dot-none = f32[1536,2048]{1,0:T(8,128)} custom-call(s32[1]{0:T(128)} %get-tuple-element.7, s32[9]{0:T(128)} %get-tuple-element.8, s32[13]{0:T(128)} %get-tuple-element.9, s32[13]{0:T(128)} %get-tuple-element.10, s32[1]{0:T(128)} %get-tuple-element.7, bf16[1536,1024]{1,0:T(8,128)(2,1)} %multiply_convert_fusion, bf16[8,1024,2048]{2,1,0:T(8,128)(2,1)} %param.13), custom_call_target="tpu_custom_call" | custom-call | flops 6442450944 | bytes 49283104 | tf_op jit(solution)/shard_map/ragged_dot_general/ragged-dot-none
  237.7 8.2 %convert_element_type.33 = bf16[1536,2048]{1,0:T(8,128)(2,1)} convert(f32[1536,2048]{1,0:T(8,128)} %ragged-dot-none) | non-fusion elementwise | flops 3145728 | bytes 18874368 | tf_op jit(solution)/shard_map/convert_element_type | solution.py:19
  245.9 19.9 %gather_fusion.3 = bf16[2048,2048]{1,0:T(8,128)(2,1)} fusion(bf16[1536,2048]{1,0:T(8,128)(2,1)} %convert_element_type.33, s32[2048]{0:T(1024)S(1)} %broadcast_clamp_fusion), kind=kCustom, calls=%fused_computation.3 | custom fusion | bytes 16785408 | tf_op jit(solution)/shard_map/gather | solution.py:74
  265.8 13.7 %all-to-all-start.2 = ((bf16[8,256,2048]{2,1,0:T(8,128)(2,1)}), bf16[8,256,2048]{2,1,0:T(8,128)(2,1)}, u32[]{:S(2)}, u32[]{:S(2)}) async-start(bf16[8,256,2048]{2,1,0:T(8,128)(2,1)} %bitcast.64), calls=%async_computation.2 | async-start | bytes 16777216 | tf_op jit(solution)/shard_map/all_to_all | solution.py:75
  279.8 4.5 %gather_fusion.4 = s32[1024]{0:T(1024)S(1)} fusion(s32[1024]{0:T(1024)S(1)} %reshape.421, s32[1024]{0:T(1024)S(1)} %get-tuple-element.23), kind=kCustom, calls=%fused_computation.4 | custom fusion | bytes 12288 | tf_op jit(solution)/shard_map/gather | solution.py:27
  284.7 7.0 %gather_fusion.6 = f32[1024]{0:T(1024)S(1)} fusion(f32[128,64]{0,1:T(8,128)S(1)} %fusion.5, s32[1024]{0:T(1024)S(1)} %reshape.495), kind=kCustom, calls=%fused_computation.6 | custom fusion | bytes 16384 | tf_op jit(solution)/shard_map/jit(take_along_axis)/gather | solution.py:66
  292.0 0.7 fusion.27
  292.7 4.4 %compare_select_fusion.11 = (s32[1024,1]{0,1:T(1,128)S(1)}, s32[1024,1]{0,1:T(1,128)S(1)}) fusion(s32[]{:T(128)} %bitcast.19, s32[]{:T(128)} %bitcast.20, s32[]{:T(128)} %bitcast.21, s32[]{:T(128)} %bitcast.22, s32[]{:T(128)} %bitcast.23, s32[]{:T(128)} %bitcast.25, s32[]{:T(128)} %bitcast.24, s32[1024,1]{0,1:T(1,128)S(1)} %bitcast.69), kind=kLoop, calls=%fused_computation.40 | loop fusion | flops 30720 | bytes 12316 | tf_op jit(solution)/shard_map/gather | solution.py:31
  297.8 4.3 %scatter_custom_fusion.2 = s32[1024]{0:T(1024)S(1)} fusion(s32[1024]{0:T(1024)S(1)} %get-tuple-element.24, s32[1024]{0:T(1024)S(1)} %fusion.17, s32[]{:T(128)} %constant.46.clone.1), kind=kCustom, calls=%fused_computation.84 | custom fusion | bytes 4100 | tf_op jit(solution)/shard_map/scatter | solution.py:32
  302.1 71.5 %all-to-all-done.2 = bf16[8,256,2048]{2,1,0:T(8,128)(2,1)} async-done(((bf16[8,256,2048]{2,1,0:T(8,128)(2,1)}), bf16[8,256,2048]{2,1,0:T(8,128)(2,1)}, u32[]{:S(2)}, u32[]{:S(2)}) %all-to-all-start.2) | async-done | bytes 8388640 | tf_op jit(solution)/shard_map/all_to_all | solution.py:75
  373.6 13.3 %gather_fusion.5 = bf16[1024,2048]{1,0:T(8,128)(2,1)} fusion(bf16[2048,2048]{1,0:T(8,128)(2,1)} %bitcast.16, s32[1024]{0:T(1024)S(1)} %fusion.18), kind=kCustom, calls=%fused_computation.5 | custom fusion | bytes 8392704 | tf_op jit(solution)/shard_map/gather | solution.py:76
  387.0 6.5 %fusion = f32[128,2048]{1,0:T(8,128)S(1)} fusion(bf16[1024,2048]{1,0:T(8,128)(2,1)} %gather_fusion.5, f32[128,8]{1,0:T(8,128)S(1)} %copy.34), kind=kLoop, calls=%fused_computation.12 | loop fusion | flops 6029312 | bytes 5246976 | tf_op jit(solution)/shard_map/reduce_sum | solution.py:77
  393.5 0.9 fusion.4
  (60 shorter events, 4.8 us)
Async XLA Ops:
  0.0 284.3 %copy-start = (bf16[2048,64]{0,1:T(8,128)(2,1)S(1)}, bf16[2048,64]{0,1:T(8,128)(2,1)}, u32[]{:S(2)}) copy-start(bf16[2048,64]{0,1:T(8,128)(2,1)} %param.10) | copy-start | bytes 786436
  0.0 29.9 %copy-start.1 = (bf16[128,2048]{1,0:T(8,128)(2,1)S(1)}, bf16[128,2048]{1,0:T(8,128)(2,1)}, u32[]{:S(2)}) copy-start(bf16[128,2048]{1,0:T(8,128)(2,1)} %param.7) | copy-start | bytes 1572868
  9.3 31.9 %all-to-all-start.1 = ((s32[8,1,8]{2,1,0:T(1,128)}), s32[8,1,8]{2,1,0:T(1,128)S(1)}, u32[]{:S(2)}, u32[]{:S(2)}) async-start(s32[8,1,8]{2,1,0:T(1,128)} %bitcast.1), calls=%async_computation.1 | async-start | bytes 8192 | tf_op jit(solution)/shard_map/all_to_all | solution.py:69
  41.1 97.7 %all-to-all-start = ((bf16[8,256,2048]{2,1,0:T(8,128)(2,1)}), bf16[8,256,2048]{2,1,0:T(8,128)(2,1)}, u32[]{:S(2)}, u32[]{:S(2)}) async-start(bf16[8,256,2048]{2,1,0:T(8,128)(2,1)} %bitcast.65), calls=%async_computation | async-start | bytes 16777216 | tf_op jit(solution)/shard_map/all_to_all | solution.py:70
  265.8 13.7 %copy-start.3 = (s32[128,8]{0,1:T(8,128)S(1)}, s32[128,8]{0,1:T(8,128)}, u32[]{:S(2)}) copy-start(s32[128,8]{0,1:T(8,128)} %param.8) | copy-start | bytes 12292
  265.8 107.8 %all-to-all-start.2 = ((bf16[8,256,2048]{2,1,0:T(8,128)(2,1)}), bf16[8,256,2048]{2,1,0:T(8,128)(2,1)}, u32[]{:S(2)}, u32[]{:S(2)}) async-start(bf16[8,256,2048]{2,1,0:T(8,128)(2,1)} %bitcast.64), calls=%async_computation.2 | async-start | bytes 16777216 | tf_op jit(solution)/shard_map/all_to_all | solution.py:75
  373.6 19.9 %copy-start.2 = (bf16[128,2048]{1,0:T(8,128)(2,1)S(1)}, bf16[128,2048]{1,0:T(8,128)(2,1)}, u32[]{:S(2)}) copy-start(bf16[128,2048]{1,0:T(8,128)(2,1)} %param.7) | copy-start | bytes 1572868
where the time goes:
time: 396 us; the launch traced here: 394 us
  waiting for transfers between devices  144 us (36%)
  local copies, waits for them, and re-layouts  106 us (27%)
  Pallas kernels  76.4 us (19%)
  other arithmetic  45.4 us (11%)
  starting transfers between devices  21.7 us (5%)
    another operation x3, Pallas kernels  74.9 us
    all_to_all x1, waiting for transfers between devices, device_step(): recv_rows = lax.all_to_all(send_rows, 'ep', 0, 0, tiled=True)  72.7 us
    all_to_all x1, waiting for transfers between devices, device_step(): home_rows = lax.all_to_all(back_rows, 'ep', 0, 0, tiled=True)  71.5 us
    gather x1, local copies, waits for them, and re-layouts, device_step(): back_rows = expert_out[back_pos].reshape(ep_size, send_max, width)  19.9 us
    gather x1, local copies, waits for them, and re-layouts, device_step(): compact_rows = recv_rows.reshape(ep_size * send_max, width)[compact_src]  17.1 us
    all_to_all x1, starting transfers between devices, device_step(): home_rows = lax.all_to_all(back_rows, 'ep', 0, 0, tiled=True)  13.7 us
    gather x1, local copies, waits for them, and re-layouts, device_step(): home_rows.reshape(ep_size * send_max, width)[slot_of_pair]  13.3 us
    gather x1, local copies, waits for them, and re-layouts, device_step(): send_rows = normed[send_tok].reshape(ep_size, send_max, width)  11 us
  transfers between devices with their start and end apart: 3, of which 2 were waited for; matrix products, arithmetic and copies ran while one was open for 18% of the time, Pallas kernels for 0%

commit v1 on v0

v1 whole, which is shorter than its diff:
```python
import functools

import jax
import jax.numpy as jnp
from jax import lax
from jax.experimental import pallas as pl
from jax.experimental.pallas import tpu as pltpu
from jax.sharding import PartitionSpec as P

NORM_EPS = 1e-5
MESH = pl.DeviceIdType.MESH
F32, BF16, I32 = jnp.float32, jnp.bfloat16, jnp.int32
FC = 128
CC = 256
WIN = 256
RG = 16


def moe_kernel(dims, x_ref, ids_ref, gain_ref, wr_ref, w1_ref, w3_ref, w2_ref, out_ref,
               xg, idsg, ug, gbuf, xs, hbuf, pbuf, gates, wa, wb, obuf, part, rd, rp1, rp2,
               meta_v, meta_s, posrow,
               s_ids, r_ids, s_own, s_fwd, r_sib, r_x, r_y, r_dg, r_sf, s_w, s_meta,
               d_s, d_r, p1_s, p1_r, p2_s, p2_r):
    T, D, FF, E, NDEV, NB = dims
    NF, NC = FF // FC, D // CC
    HT = T // 2
    me = lax.axis_index('ep')
    core = me % 2
    cx = (me // 2) % 2
    cy = me // 4
    sib = cy * 4 + cx * 2 + (1 - core)
    xn = cy * 4 + (1 - cx) * 2 + core
    yn = (1 - cy) * 4 + cx * 2 + core
    dg = (1 - cy) * 4 + (1 - cx) * 2 + core

    def remote(src, dst, ss, rs, dev):
        return pltpu.make_async_remote_copy(src_ref=src, dst_ref=dst, send_sem=ss, recv_sem=rs,
                                            device_id={'ep': dev}, device_id_type=MESH)

    wslots = (wa, wb)

    def a_copies(f, slot):
        cols = pl.ds(pl.multiple_of(f * FC, FC), FC)
        return (pltpu.make_async_copy(w1_ref.at[:, :, cols], wslots[slot].at[:, :, pl.ds(0, FC)], s_w.at[slot, 0]),
                pltpu.make_async_copy(w3_ref.at[:, :, cols], wslots[slot].at[:, :, pl.ds(FC, FC)], s_w.at[slot, 1]))

    def b_copy(c, slot, half):
        cols = pl.ds(pl.multiple_of(c * CC, CC), CC)
        rows = pl.ds(pl.multiple_of(half * FF, FF), FF)
        return pltpu.make_async_copy(w2_ref.at[:, :, cols], wslots[slot].at[:, rows, :], s_w.at[slot, half])

    for slot in range(2):
        for cp in a_copies(slot, slot):
            cp.start()

    barrier = pltpu.get_barrier_semaphore()
    for k in range(1, NDEV):
        pl.semaphore_signal(barrier, inc=1, device_id={'ep': (me + k) % NDEV}, device_id_type=MESH)
    pl.semaphore_wait(barrier, NDEV - 1)

    def ids_copy(k):
        return remote(ids_ref, idsg.at[me], s_ids.at[k - 1], r_ids.at[k - 1], (me + k) % NDEV)

    for k in range(1, NDEV):
        ids_copy(k).start()
    own_sib = remote(x_ref, xg.at[me], s_own.at[0], r_sib, sib)
    h0, h1 = pl.ds(0, HT), pl.ds(HT, HT)
    halves = (h0, h1)

    def own_x(h):
        return remote(x_ref.at[halves[h], :], xg.at[me, halves[h], :], s_own.at[1 + h], r_x.at[h], xn)

    def own_y(h):
        return remote(x_ref.at[halves[h], :], xg.at[me, halves[h], :], s_own.at[3 + h], r_y.at[h], yn)

    own_x(0).start()
    own_y(1).start()
    own_x(1).start()
    own_y(0).start()
    own_sib.start()

    def norm_rows(src, row0):
        def body(i, carry):
            rows = pl.ds(pl.multiple_of(i * 16, 16), 16)
            t = src[rows, :].astype(F32)
            inv = lax.rsqrt(jnp.mean(t * t, axis=1, keepdims=True) + NORM_EPS)
            ug[pl.ds(pl.multiple_of(row0 + i * 16, 16), 16), :] = (t * inv * gain_ref[...].astype(F32)).astype(BF16)
            return carry
        lax.fori_loop(0, T // 16, body, 0)

    norm_rows(x_ref, core * T)

    idsg[me] = ids_ref[...]
    for k in range(1, NDEV):
        ids_copy(k).wait_recv()
    sub_e = lax.broadcasted_iota(I32, (E, T), 0)
    lane = lax.broadcasted_iota(I32, (E, T), 1)
    masks = []
    for s in range(NDEV):
        ids = idsg[s]
        m = jnp.zeros((E, T), I32)
        for j in range(ids.shape[0]):
            m = m + (ids[j:j + 1, :] == sub_e + me * E).astype(I32)
        masks.append(m)
    tri = (lax.broadcasted_iota(I32, (T, T), 0) <= lax.broadcasted_iota(I32, (T, T), 1)).astype(F32).astype(BF16)
    counts = [jnp.sum(m, axis=1, keepdims=True) for m in masks]
    total = counts[0]
    for s in range(1, NDEV):
        total = total + counts[s]
    nblk = (total + (T - 1)) // T
    nblk = jnp.broadcast_to(nblk, (E, T))
    start = jnp.zeros((E, T), I32)
    for e in range(E - 1):
        start = start + jnp.where(sub_e > e, jnp.broadcast_to(nblk[e:e + 1, :], (E, T)), 0)
    eid = jnp.sum((start + nblk <= lane).astype(I32), axis=0, keepdims=True)
    eid = jnp.minimum(eid, E - 1)
    base = start * T
    wst = jnp.zeros((E, T), I32)
    poss = []
    for s in range(NDEV):
        rank = jnp.dot(masks[s].astype(F32).astype(BF16), tri, preferred_element_type=F32).astype(I32)
        pos = jnp.where(masks[s] > 0, base + rank - 1, -1)
        poss.append(pos)
        for e in range(E):
            posrow[e, s] = jnp.broadcast_to(pos[e:e + 1, :], (8, T))
        w0 = jnp.minimum(base // RG, (NB * T - WIN) // RG)
        wst = wst + jnp.where(lane == s, w0, 0)
        base = base + counts[s]
    meta_v[0:E, :] = wst
    meta_v[E:2 * E, :] = jnp.broadcast_to(eid, (E, T))
    meta_copy = pltpu.make_async_copy(meta_v, meta_s, s_meta)
    meta_copy.start()
    meta_copy.wait()
    wlane = lax.broadcasted_iota(I32, (T, WIN), 1)
    for s in range(NDEV):
        padded = jnp.concatenate([poss[s], jnp.zeros((T - E, T), I32)], axis=0).astype(F32)
        col = padded.T
        for e in range(E):
            pc = col[:, e:e + 1].astype(I32)
            pbuf[s, e] = (pc == wlane + meta_s[e, s] * RG).astype(F32).astype(BF16)

    def route_chip(chip, first):
        logits = jnp.dot(ug[...], wr_ref[...], preferred_element_type=F32)
        both = jnp.concatenate([logits, logits], axis=1)
        ex = jnp.exp(both - jnp.max(both, axis=1, keepdims=True))
        prob = ex / (jnp.sum(ex, axis=1, keepdims=True) * 0.5)
        prob = pltpu.roll(prob, (128 - me * E) % 128, 1)
        gates[chip * 2] = prob[:T]
        gates[chip * 2 + 1] = prob[T:]

        def build(b, carry):
            e = meta_s[E, b]
            rows = lax.broadcasted_iota(I32, (T, T), 0) + b * T
            for c in range(2):
                p = jnp.broadcast_to(posrow[e, chip * 2 + c][0:1, :], (T, T))
                gbuf[pl.ds(pl.multiple_of(b * T, T), T), c * T:(c + 1) * T] = (p == rows).astype(F32).astype(BF16)
            return carry
        lax.fori_loop(0, NB, build, 0)
        MR = NB * T // 4

        def gather(i, carry):
            rows = pl.ds(pl.multiple_of((i // 4) * MR, 16), MR)
            cols = pl.ds(pl.multiple_of((i % 4) * (D // 4), 128), D // 4)
            got = jnp.dot(gbuf[rows, :], ug[:, cols], preferred_element_type=F32).astype(BF16)
            if first:
                xs[rows, cols] = got
            else:
                xs[rows, cols] = xs[rows, cols] + got
            return carry
        lax.fori_loop(0, 16, gather, 0)

    def sib_fwd(kind, h, src_dev):
        return remote(xg.at[src_dev, halves[h], :], xg.at[src_dev, halves[h], :],
                      s_fwd.at[2 + kind * 2 + h], r_sf.at[kind, h], sib)

    own_sib.wait_recv()
    norm_rows(xg.at[sib], (1 - core) * T)
    route_chip(cy * 2 + cx, True)

    own_x(0).wait_recv()
    fwd_y = remote(xg.at[xn, h0, :], xg.at[xn, h0, :], s_fwd.at[0], r_dg.at[0], yn)
    fwd_y.start()
    sib_fwd(0, 0, xn).start()
    own_y(1).wait_recv()
    fwd_x = remote(xg.at[yn, h1, :], xg.at[yn, h1, :], s_fwd.at[1], r_dg.at[1], xn)
    fwd_x.start()
    sib_fwd(1, 1, yn).start()
    own_x(1).wait_recv()
    sib_fwd(0, 1, xn).start()
    own_y(0).wait_recv()
    sib_fwd(1, 0, yn).start()

    def take(kind, dev, chip):
        norm_rows(xg.at[dev], core * T)
        other = dev + 1 - 2 * core
        for h in range(2):
            sib_fwd(kind, h, dev).wait_recv()
        norm_rows(xg.at[other], (1 - core) * T)
        route_chip(chip, False)

    take(0, xn, cy * 2 + (1 - cx))
    take(1, yn, (1 - cy) * 2 + cx)
    fwd_y.wait_recv()
    sib_fwd(2, 0, dg).start()
    fwd_x.wait_recv()
    sib_fwd(2, 1, dg).start()
    take(2, dg, (1 - cy) * 2 + (1 - cx))

    def hidden(g, carry):
        for slot in range(2):
            f = g * 2 + slot
            for cp in a_copies(f, slot):
                cp.wait()
            cols = pl.ds(pl.multiple_of(f * FC, FC), FC)
            for b in range(NB):
                e = meta_s[E, b]
                acc = jnp.dot(xs[b * T:(b + 1) * T, :], wslots[slot][e], preferred_element_type=F32)
                hg, hu = acc[:, :FC], acc[:, FC:]
                hbuf[b * T:(b + 1) * T, cols] = (jax.nn.silu(hg) * hu).astype(BF16)

            @pl.when(g < NF // 2 - 1)
            def _():
                for cp in a_copies(f + 2, slot):
                    cp.start()

            @pl.when(g >= NF // 2 - 1)
            def _():
                for h in range(2):
                    b_copy(slot * 2 + h, slot, h).start()
        return carry

    lax.fori_loop(0, NF // 2, hidden, 0)

    def d2d(j):
        return remote(part.at[j % 4, 1 - core], rd.at[j], d_s.at[j], d_r.at[j], sib)

    def first_hop(j):
        return (remote(part.at[j % 4, core, 0, :, 1 - cx], rp1.at[j, 0], p1_s.at[j, 0], p1_r.at[j, 0], xn),
                remote(part.at[j % 4, core, 1, 1 - cy], rp1.at[j, 1], p1_s.at[j, 1], p1_r.at[j, 1], yn))

    def second_hop(j):
        return (remote(part.at[j % 4, core, 0, 1 - cy, cx], rp2.at[j, 0], p2_s.at[j, 0], p2_r.at[j, 0], yn),
                remote(part.at[j % 4, core, 1, cy, 1 - cx], rp2.at[j, 1], p2_s.at[j, 1], p2_r.at[j, 1], xn))

    def combine(c, to_core):
        for ch in range(NDEV // 2):
            s = ch * 2 + to_core
            acc = jnp.zeros((T, CC), F32)
            for e in range(E):
                r0 = meta_s[e, s]
                rows = jnp.concatenate([obuf[r0 + k] for k in range(WIN // RG)], axis=0)
                got = jnp.dot(pbuf[s, e], rows, preferred_element_type=F32)
                acc = acc + gates[s, :, e:e + 1] * got
            for h in range(2):
                part[c % 4, to_core, h, ch // 2, ch % 2] = acc[:, h * 128:(h + 1) * 128]

    def outputs(i, half, slot):
        rows = pl.ds(pl.multiple_of(half * FF, FF), FF)
        for b in range(NB):
            e = meta_s[E, b]
            acc = jnp.dot(hbuf[b * T:(b + 1) * T, :], wslots[slot][e, rows, :], preferred_element_type=F32)
            obuf[b * (T // RG):(b + 1) * (T // RG)] = acc.astype(BF16).reshape(T // RG, RG, CC)
        combine(i, 1 - core)
        d2d(i).start()
        combine(i, core)

    def drain(i):
        @pl.when((i >= 1) & (i < NC + 1))
        def _():
            j = i - 1
            d2d(j).wait_recv()
            for h in range(2):
                for ch in range(NDEV // 2):
                    at = (j % 4, core, h, ch // 2, ch % 2)
                    part[at] = part[at] + rd[j, h, ch // 2, ch % 2]
            for cp in first_hop(j):
                cp.start()

        @pl.when((i >= 2) & (i < NC + 2))
        def _():
            j = i - 2
            for h, cp in enumerate(first_hop(j)):
                cp.wait_recv()
                for k in range(2):
                    at = (j % 4, core, h, k, cx) if h == 0 else (j % 4, core, h, cy, k)
                    part[at] = part[at] + rp1[j, h, k]
            for cp in second_hop(j):
                cp.start()

        @pl.when(i >= 3)
        def _():
            j = i - 3
            for h, cp in enumerate(second_hop(j)):
                cp.wait_recv()
                cols = pl.ds(pl.multiple_of(j * CC + h * 128, 128), 128)
                moe = part[j % 4, core, h, cy, cx] + rp2[j, h]
                out_ref[:, cols] = (x_ref[:, cols].astype(F32) + moe).astype(BF16)
            d2d(j).wait_send()
            for cp in first_hop(j):
                cp.wait_send()
            for cp in second_hop(j):
                cp.wait_send()

    def four(g, carry):
        for slot in range(2):
            for h in range(2):
                b_copy(g * 4 + slot * 2 + h, slot, h).wait()

            def two(half, inner):
                i = g * 4 + slot * 2 + half
                outputs(i, half, slot)
                drain(i)
                return inner
            lax.fori_loop(0, 2, two, 0)

            @pl.when(g < NC // 4 - 1)
            def _():
                for h in range(2):
                    b_copy((g + 1) * 4 + slot * 2 + h, slot, h).start()
        return carry

    lax.fori_loop(0, NC // 4, four, 0)

    def last(i, carry):
        drain(i)
        return carry

    lax.fori_loop(NC, NC + 3, last, 0)

    for k in range(1, NDEV):
        ids_copy(k).wait_send()
    own_sib.wait_send()
    for h in range(2):
        own_x(h).wait_send()
        own_y(h).wait_send()
    fwd_y.wait_send()
    fwd_x.wait_send()
    for kind, dev in enumerate((xn, yn, dg)):
        for h in range(2):
            sib_fwd(kind, h, dev).wait_send()


def solution(mesh):
    ndev = mesh.shape['ep']

    def device_step(tokens, expert_ids, norm_gain, w_router, w_gate, w_up, w_down):
        T, D = tokens.shape
        top = expert_ids.shape[1]
        E, _, FF = w_gate.shape
        NR = w_router.shape[1]
        most = 3 * T * top // 2
        NB = (most + E * (T - 1)) // T
        NC = D // CC
        dims = (T, D, FF, E, ndev, NB)
        vmem = pl.BlockSpec(memory_space=pltpu.VMEM)
        hbm = pl.BlockSpec(memory_space=pl.ANY)
        dma = pltpu.SemaphoreType.DMA
        return pl.pallas_call(
            functools.partial(moe_kernel, dims),
            out_shape=jax.ShapeDtypeStruct((T, D), BF16),
            in_specs=[vmem, vmem, vmem, vmem, hbm, hbm, hbm],
            out_specs=vmem,
            scratch_shapes=[
                pltpu.VMEM((ndev, T, D), BF16),
                pltpu.VMEM((ndev, top, T), I32),
                pltpu.VMEM((2 * T, D), BF16),
                pltpu.VMEM((NB * T, 2 * T), BF16),
                pltpu.VMEM((NB * T, D), BF16),
                pltpu.VMEM((NB * T, FF), BF16),
                pltpu.VMEM((ndev, E, T, WIN), BF16),
                pltpu.VMEM((ndev, T, 128), F32),
                pltpu.VMEM((E, D, 2 * FC), BF16),
                pltpu.VMEM((E, D, 2 * FC), BF16),
                pltpu.VMEM((NB * T // RG, RG, CC), BF16),
                pltpu.VMEM((4, 2, 2, 2, 2, T, 128), F32),
                pltpu.VMEM((NC, 2, 2, 2, T, 128), F32),
                pltpu.VMEM((NC, 2, 2, T, 128), F32),
                pltpu.VMEM((NC, 2, T, 128), F32),
                pltpu.VMEM((2 * E, T), I32),
                pltpu.SMEM((2 * E, T), I32),
                pltpu.VMEM((E, ndev, 8, T), I32),
                dma((ndev - 1,)), dma((ndev - 1,)),
                dma((5,)), dma((8,)),
                dma, dma((2,)), dma((2,)), dma((2,)), dma((3, 2)),
                dma((2, 2)), dma,
                dma((NC,)), dma((NC,)), dma((NC, 2)), dma((NC, 2)), dma((NC, 2)), dma((NC, 2)),
            ],
            compiler_params=pltpu.CompilerParams(
                collective_id=0, has_side_effects=True, vmem_limit_bytes=67043328),
            name='moe_block',
        )(tokens, expert_ids.T, norm_gain.reshape(1, D), w_router, w_gate, w_up, w_down)

    row_spec = P(('dp', 'ep'), None)
    expert_spec = P('ep', None, None)
    return jax.shard_map(device_step, mesh=mesh,
                         in_specs=(row_spec, row_spec, P(None), P(None, None), expert_spec, expert_spec, expert_spec),
                         out_specs=row_spec, check_vma=False)
```

time: 396 us -> 122 us (0.31)
  waiting for transfers between devices: 144 us -> 0 us
  local copies, waits for them, and re-layouts: 106 us -> 5.12 us
  other arithmetic: 45.4 us -> 0 us
  Pallas kernels: 76.4 us -> 117 us
  starting transfers between devices: 21.7 us -> 0 us
    all_to_all x3 -> x0, waiting for transfers between devices: 144 us -> none  [the longest x1 72.7 us: device_step(): recv_rows = lax.all_to_all(send_rows, 'ep', 0, 0, tiled=True)]
    pallas_call x0 -> x1, Pallas kernels: none -> 117 us  [device_step(): pl.pallas_call(functools.partial(moe_kernel, dims), out_shape=jax.ShapeDt...]
    gather x13 -> x0, local copies, waits for them, and re-layouts: 91.7 us -> none  [the longest x1 19.9 us: device_step(): back_rows = expert_out[back_pos].reshape(ep_size, send_max, width)]
    another operation x3 -> x0, Pallas kernels: 74.9 us -> none
    all_to_all x3 -> x0, starting transfers between devices: 21.7 us -> none  [the longest x1 13.7 us: device_step(): home_rows = lax.all_to_all(back_rows, 'ep', 0, 0, tiled=True)]
    convert_element_type x5 -> x0, other arithmetic: 16.9 us -> none  [the longest x1 8.22 us: expert_ffn(): lax.ragged_dot(swiglu_out, w_down, group_sizes, preferred_element_type=jn...]
    scatter x2 -> x0, local copies, waits for them, and re-layouts: 12.4 us -> none  [the longest x1 8.05 us: recv_plan(): jnp.zeros((recv_max,), jnp.int32).at[compact_pos]]
    reduce_sum x6 -> x0, other arithmetic: 8.53 us -> none  [the longest x1 6.52 us: device_step(): moe_sum = jnp.sum(gate_vals[:, :, None] * pair_out, axis=1)]
  transfers between devices with their start and end apart: 3 -> 0, of which waited for: 2 -> 0; matrix products, arithmetic and copies ran while one was open for 18% -> 0% of each run, Pallas kernels for 0% -> 0%
where the time goes in v1:
time: 122 us
  Pallas kernels  117 us (96%)
  local copies, waits for them, and re-layouts  5.12 us (4%)
    pallas_call x1, Pallas kernels, device_step(): pl.pallas_call(functools.partial(moe_kernel, dims), out_shape=jax.ShapeDt...  117 us
    unnamed x2, local copies, waits for them, and re-layouts  3.83 us

profile of v1, /device:TPU:0, one launch (start us, length us, event | category | flops | bytes accessed | tf_op | source)
XLA Modules:
  0.0 122.0 jit_solution(10942695601443123450)
XLA Ops:
  0.0 1.3 %reshape.3.gain_ref = bf16[1,2048]{1,0:T(2,128)(2,1)} reshape(bf16[2048]{0:T(1024)(128)(2,1)} %param.9) | data formatting | bytes 8192 | tf_op jit(solution)/shard_map/reshape | solution.py:391
  1.3 2.0 %copy.8.wr_ref = bf16[2048,64]{1,0:T(8,128)(2,1)} copy(bf16[2048,64]{0,1:T(8,128)(2,1)} %param.10) | data formatting | bytes 524288 | tf_op args[3]
  3.2 116.9 %moe_block.1 = bf16[128,2048]{1,0:T(8,128)(2,1)} custom-call(bf16[128,2048]{1,0:T(8,128)(2,1)} %x_ref.1, s32[8,128]{1,0:T(8,128)} %bitcast.1, bf16[1,2048]{1,0:T(2,128)(2,1)} %reshape.3.gain_ref, bf16[2048,64]{1,0:T(8,128)(2,1)} %copy.8.wr_ref, bf16[8,2048,1024]{2,1,0:T(8,128)(2,1)} %w1_ref.1, bf16[8,2048,1024]{2,1,0:T(8,128)(2,1)} %w3_ref.1, ...), custom_call_target="tpu_custom_call" | custom-call | tf_op jit(solution)/shard_map/moe_block/pallas_call | solution.py:358
  120.1 1.9 %copy.10 = bf16[128,2048]{1,0:T(8,128)(2,1)} copy(bf16[128,2048]{1,0:T(8,128)(2,1)} %moe_block.1) | data formatting | bytes 1048576

commit v2 on v1

--- a/solution.py
+++ b/solution.py
@@ -12,14 +12,15 @@
 F32, BF16, I32 = jnp.float32, jnp.bfloat16, jnp.int32
 FC = 128
 CC = 256
+NQ = 4
 WIN = 256
 RG = 16
 
 
 def moe_kernel(dims, x_ref, ids_ref, gain_ref, wr_ref, w1_ref, w3_ref, w2_ref, out_ref,
-               xg, idsg, ug, gbuf, xs, hbuf, pbuf, gates, wa, wb, obuf, part, rd, rp1, rp2,
+               xg, idsg, gsrc, gdst, gbuf, xs, hbuf, pbuf, gates, wa, wb, obuf, part, rd, rp1, rp2,
                meta_v, meta_s, posrow,
-               s_ids, r_ids, s_own, s_fwd, r_sib, r_x, r_y, r_dg, r_sf, s_w, s_meta,
+               s_ids, r_ids, s_gt, r_gt, s_sib, r_sib, s_nb, r_nb, s_dg, r_dg, s_sf, r_sf, s_sd, r_sd, s_w, s_meta,
                d_s, d_r, p1_s, p1_r, p2_s, p2_r):
     T, D, FF, E, NDEV, NB = dims
     NF, NC = FF // FC, D // CC
@@ -31,7 +32,6 @@
     sib = cy * 4 + cx * 2 + (1 - core)
     xn = cy * 4 + (1 - cx) * 2 + core
     yn = (1 - cy) * 4 + cx * 2 + core
-    dg = (1 - cy) * 4 + (1 - cx) * 2 + core
 
     def remote(src, dst, ss, rs, dev):
         return pltpu.make_async_remote_copy(src_ref=src, dst_ref=dst, send_sem=ss, recv_sem=rs,
@@ -56,39 +56,68 @@
     barrier = pltpu.get_barrier_semaphore()
     for k in range(1, NDEV):
         pl.semaphore_signal(barrier, inc=1, device_id={'ep': (me + k) % NDEV}, device_id_type=MESH)
+
+    own = xg.at[me // 2, core]
+
+    def norm_rows(i, carry):
+        rows = pl.ds(pl.multiple_of(i * 16, 16), 16)
+        t = x_ref[rows, :].astype(F32)
+        inv = lax.rsqrt(jnp.mean(t * t, axis=1, keepdims=True) + NORM_EPS)
+        xg[me // 2, core, rows, :] = (t * inv * gain_ref[...].astype(F32).reshape(1, D)).astype(BF16)
+        return carry
+
+    lax.fori_loop(0, T // 16, norm_rows, 0)
     pl.semaphore_wait(barrier, NDEV - 1)
 
     def ids_copy(k):
         return remote(ids_ref, idsg.at[me], s_ids.at[k - 1], r_ids.at[k - 1], (me + k) % NDEV)
 
+    def gate_copy(k):
+        to = (me + k) % NDEV
+        return remote(gsrc.at[to], gdst.at[me], s_gt.at[k - 1], r_gt.at[k - 1], to)
+
+    chip_x = cy * 2 + (1 - cx)
+    chip_y = (1 - cy) * 2 + cx
+    chip_d = (1 - cy) * 2 + (1 - cx)
+    chip_me = cy * 2 + cx
+    QC = D // NQ
+
+    def part_of(chip, q, rows=pl.ds(0, T)):
+        return xg.at[chip, core, rows, pl.ds(q * QC, QC)]
+
+    def to_sib(q):
+        return remote(part_of(chip_me, q), part_of(chip_me, q), s_sib.at[q], r_sib.at[q], sib)
+
+    def to_nb(k, q):
+        return remote(part_of(chip_me, q), part_of(chip_me, q), s_nb.at[k, q], r_nb.at[k, q], (xn, yn)[k])
+
+    halves = (pl.ds(0, HT), pl.ds(HT, HT))
+
+    def to_diag(k, q):
+        src = part_of((chip_x, chip_y)[k], q, halves[k])
+        return remote(src, src, s_dg.at[k, q], r_dg.at[k, q], (yn, xn)[k])
+
+    def nb_sib(k, q):
+        src = part_of((chip_x, chip_y)[k], q)
+        return remote(src, src, s_sf.at[k, q], r_sf.at[k, q], sib)
+
+    def diag_sib(k, q):
+        src = part_of(chip_d, q, halves[k])
+        return remote(src, src, s_sd.at[k, q], r_sd.at[k, q], sib)
+
     for k in range(1, NDEV):
         ids_copy(k).start()
-    own_sib = remote(x_ref, xg.at[me], s_own.at[0], r_sib, sib)
-    h0, h1 = pl.ds(0, HT), pl.ds(HT, HT)
-    halves = (h0, h1)
-
-    def own_x(h):
-        return remote(x_ref.at[halves[h], :], xg.at[me, halves[h], :], s_own.at[1 + h], r_x.at[h], xn)
-
-    def own_y(h):
-        return remote(x_ref.at[halves[h], :], xg.at[me, halves[h], :], s_own.at[3 + h], r_y.at[h], yn)
-
-    own_x(0).start()
-    own_y(1).start()
-    own_x(1).start()
-    own_y(0).start()
-    own_sib.start()
-
-    def norm_rows(src, row0):
-        def body(i, carry):
-            rows = pl.ds(pl.multiple_of(i * 16, 16), 16)
-            t = src[rows, :].astype(F32)
-            inv = lax.rsqrt(jnp.mean(t * t, axis=1, keepdims=True) + NORM_EPS)
-            ug[pl.ds(pl.multiple_of(row0 + i * 16, 16), 16), :] = (t * inv * gain_ref[...].astype(F32)).astype(BF16)
-            return carry
-        lax.fori_loop(0, T // 16, body, 0)
-
-    norm_rows(x_ref, core * T)
+    for q in range(NQ):
+        to_nb(0, q).start()
+        to_nb(1, q).start()
+        to_sib(q).start()
+
+    logits = lax.dot_general(wr_ref[...], own[...], (((1,), (1,)), ((), ())), preferred_element_type=F32)
+    ex = jnp.exp(logits - jnp.max(logits, axis=0, keepdims=True))
+    prob = ex / jnp.sum(ex, axis=0, keepdims=True)
+    for r in range(NDEV):
+        gsrc[r] = prob[r * E:(r + 1) * E]
+    gdst[me] = gsrc[me]
 
     idsg[me] = ids_ref[...]
     for k in range(1, NDEV):
@@ -131,80 +160,67 @@
     meta_copy = pltpu.make_async_copy(meta_v, meta_s, s_meta)
     meta_copy.start()
     meta_copy.wait()
+    for k in range(1, NDEV):
+        gate_copy(k).start()
+
+    def build(b, carry):
+        e = meta_s[E, b]
+        rows = lax.broadcasted_iota(I32, (T, T), 0) + b * T
+        for s in range(NDEV):
+            p = jnp.broadcast_to(posrow[e, s][0:1, :], (T, T))
+            gbuf[s // 2, pl.ds(pl.multiple_of(b * T, T), T), (s % 2) * T:(s % 2 + 1) * T] = (p == rows).astype(F32).astype(BF16)
+        return carry
+
+    lax.fori_loop(0, NB, build, 0)
+    MR = NB * T // 4
+
+    def gather(q, chips, add):
+        cols = pl.ds(q * QC, QC)
+
+        def body(i, carry):
+            rows = pl.ds(pl.multiple_of(i * MR, 16), MR)
+            got = None
+            for chip in chips:
+                one = jnp.dot(gbuf[chip, rows, :], xg[chip, :, :, cols].reshape(2 * T, QC), preferred_element_type=F32)
+                got = one if got is None else got + one
+            got = got.astype(BF16)
+            xs[rows, cols] = xs[rows, cols] + got if add else got
+            return carry
+        lax.fori_loop(0, 4, body, 0)
+
+    for q in range(NQ):
+        for k in range(2):
+            to_nb(k, q).wait_recv()
+            to_diag(k, q).start()
+            nb_sib(k, q).start()
+        if q > 0:
+            gather(q - 1, (chip_me, chip_x, chip_y), False)
+        to_sib(q).wait_recv()
+        for k in range(2):
+            nb_sib(k, q).wait_recv()
+    gather(NQ - 1, (chip_me, chip_x, chip_y), False)
+
     wlane = lax.broadcasted_iota(I32, (T, WIN), 1)
-    for s in range(NDEV):
+
+    def windows(s):
         padded = jnp.concatenate([poss[s], jnp.zeros((T - E, T), I32)], axis=0).astype(F32)
         col = padded.T
         for e in range(E):
             pc = col[:, e:e + 1].astype(I32)
             pbuf[s, e] = (pc == wlane + meta_s[e, s] * RG).astype(F32).astype(BF16)
-
-    def route_chip(chip, first):
-        logits = jnp.dot(ug[...], wr_ref[...], preferred_element_type=F32)
-        both = jnp.concatenate([logits, logits], axis=1)
-        ex = jnp.exp(both - jnp.max(both, axis=1, keepdims=True))
-        prob = ex / (jnp.sum(ex, axis=1, keepdims=True) * 0.5)
-        prob = pltpu.roll(prob, (128 - me * E) % 128, 1)
-        gates[chip * 2] = prob[:T]
-        gates[chip * 2 + 1] = prob[T:]
-
-        def build(b, carry):
-            e = meta_s[E, b]
-            rows = lax.broadcasted_iota(I32, (T, T), 0) + b * T
-            for c in range(2):
-                p = jnp.broadcast_to(posrow[e, chip * 2 + c][0:1, :], (T, T))
-                gbuf[pl.ds(pl.multiple_of(b * T, T), T), c * T:(c + 1) * T] = (p == rows).astype(F32).astype(BF16)
-            return carry
-        lax.fori_loop(0, NB, build, 0)
-        MR = NB * T // 4
-
-        def gather(i, carry):
-            rows = pl.ds(pl.multiple_of((i // 4) * MR, 16), MR)
-            cols = pl.ds(pl.multiple_of((i % 4) * (D // 4), 128), D // 4)
-            got = jnp.dot(gbuf[rows, :], ug[:, cols], preferred_element_type=F32).astype(BF16)
-            if first:
-                xs[rows, cols] = got
-            else:
-                xs[rows, cols] = xs[rows, cols] + got
-            return carry
-        lax.fori_loop(0, 16, gather, 0)
-
-    def sib_fwd(kind, h, src_dev):
-        return remote(xg.at[src_dev, halves[h], :], xg.at[src_dev, halves[h], :],
-                      s_fwd.at[2 + kind * 2 + h], r_sf.at[kind, h], sib)
-
-    own_sib.wait_recv()
-    norm_rows(xg.at[sib], (1 - core) * T)
-    route_chip(cy * 2 + cx, True)
-
-    own_x(0).wait_recv()
-    fwd_y = remote(xg.at[xn, h0, :], xg.at[xn, h0, :], s_fwd.at[0], r_dg.at[0], yn)
-    fwd_y.start()
-    sib_fwd(0, 0, xn).start()
-    own_y(1).wait_recv()
-    fwd_x = remote(xg.at[yn, h1, :], xg.at[yn, h1, :], s_fwd.at[1], r_dg.at[1], xn)
-    fwd_x.start()
-    sib_fwd(1, 1, yn).start()
-    own_x(1).wait_recv()
-    sib_fwd(0, 1, xn).start()
-    own_y(0).wait_recv()
-    sib_fwd(1, 0, yn).start()
-
-    def take(kind, dev, chip):
-        norm_rows(xg.at[dev], core * T)
-        other = dev + 1 - 2 * core
-        for h in range(2):
-            sib_fwd(kind, h, dev).wait_recv()
-        norm_rows(xg.at[other], (1 - core) * T)
-        route_chip(chip, False)
-
-    take(0, xn, cy * 2 + (1 - cx))
-    take(1, yn, (1 - cy) * 2 + cx)
-    fwd_y.wait_recv()
-    sib_fwd(2, 0, dg).start()
-    fwd_x.wait_recv()
-    sib_fwd(2, 1, dg).start()
-    take(2, dg, (1 - cy) * 2 + (1 - cx))
+        gates[s] = jnp.concatenate([gdst[s], jnp.zeros((T - E, T), F32)], axis=0).T
+
+    for k in range(1, NDEV):
+        gate_copy(k).wait_recv()
+    for q in range(NQ):
+        for k in range(2):
+            to_diag(k, q).wait_recv()
+            diag_sib(k, q).start()
+        windows(2 * q)
+        windows(2 * q + 1)
+        for k in range(2):
+            diag_sib(k, q).wait_recv()
+        gather(q, (chip_d,), True)
 
     def hidden(g, carry):
         for slot in range(2):
@@ -329,15 +345,12 @@
 
     for k in range(1, NDEV):
         ids_copy(k).wait_send()
-    own_sib.wait_send()
-    for h in range(2):
-        own_x(h).wait_send()
-        own_y(h).wait_send()
-    fwd_y.wait_send()
-    fwd_x.wait_send()
-    for kind, dev in enumerate((xn, yn, dg)):
-        for h in range(2):
-            sib_fwd(kind, h, dev).wait_send()
+        gate_copy(k).wait_send()
+    for q in range(NQ):
+        to_sib(q).wait_send()
+        for k in range(2):
+            for move in (to_nb, to_diag, nb_sib, diag_sib):
+                move(k, q).wait_send()
 
 
 def solution(mesh):
@@ -347,7 +360,6 @@
         T, D = tokens.shape
         top = expert_ids.shape[1]
         E, _, FF = w_gate.shape
-        NR = w_router.shape[1]
         most = 3 * T * top // 2
         NB = (most + E * (T - 1)) // T
         NC = D // CC
@@ -361,10 +373,11 @@
             in_specs=[vmem, vmem, vmem, vmem, hbm, hbm, hbm],
             out_specs=vmem,
             scratch_shapes=[
-                pltpu.VMEM((ndev, T, D), BF16),
+                pltpu.VMEM((ndev // 2, 2, T, D), BF16),
                 pltpu.VMEM((ndev, top, T), I32),
-                pltpu.VMEM((2 * T, D), BF16),
-                pltpu.VMEM((NB * T, 2 * T), BF16),
+                pltpu.VMEM((ndev, E, T), F32),
+                pltpu.VMEM((ndev, E, T), F32),
+                pltpu.VMEM((ndev // 2, NB * T, 2 * T), BF16),
                 pltpu.VMEM((NB * T, D), BF16),
                 pltpu.VMEM((NB * T, FF), BF16),
                 pltpu.VMEM((ndev, E, T, WIN), BF16),
@@ -380,15 +393,16 @@
                 pltpu.SMEM((2 * E, T), I32),
                 pltpu.VMEM((E, ndev, 8, T), I32),
                 dma((ndev - 1,)), dma((ndev - 1,)),
-                dma((5,)), dma((8,)),
-                dma, dma((2,)), dma((2,)), dma((2,)), dma((3, 2)),
+                dma((ndev - 1,)), dma((ndev - 1,)),
+                dma((NQ,)), dma((NQ,)), dma((2, NQ)), dma((2, NQ)),
+                dma((2, NQ)), dma((2, NQ)), dma((2, NQ)), dma((2, NQ)), dma((2, NQ)), dma((2, NQ)),
                 dma((2, 2)), dma,
                 dma((NC,)), dma((NC,)), dma((NC, 2)), dma((NC, 2)), dma((NC, 2)), dma((NC, 2)),
             ],
             compiler_params=pltpu.CompilerParams(
                 collective_id=0, has_side_effects=True, vmem_limit_bytes=67043328),
             name='moe_block',
-        )(tokens, expert_ids.T, norm_gain.reshape(1, D), w_router, w_gate, w_up, w_down)
+        )(tokens, expert_ids.T, norm_gain, w_router.T, w_gate, w_up, w_down)
 
     row_spec = P(('dp', 'ep'), None)
     expert_spec = P('ep', None, None)

time: 122 us -> 109 us (0.89)
  Pallas kernels: 117 us -> 107 us
  local copies, waits for them, and re-layouts: 5.12 us -> 1.88 us
    pallas_call x1, Pallas kernels: 117 us -> 107 us  [device_step(): pl.pallas_call(functools.partial(moe_kernel, dims), out_shape=jax.ShapeDt...]
    unnamed x2 -> x1, local copies, waits for them, and re-layouts: 3.83 us -> 1.88 us
    reshape x1 -> x0, local copies, waits for them, and re-layouts: 1.28 us -> none  [device_step(): norm_gain.reshape(1, D)]
where the time goes in v2:
time: 109 us
  Pallas kernels  107 us (98%)
  local copies, waits for them, and re-layouts  1.88 us (2%)
    pallas_call x1, Pallas kernels, device_step(): pl.pallas_call(functools.partial(moe_kernel, dims), out_shape=jax.ShapeDt...  107 us

profile of v2, /device:TPU:0, one launch (start us, length us, event | category | flops | bytes accessed | tf_op | source)
XLA Modules:
  0.0 108.9 jit_solution(1196452959651774773)
XLA Ops:
  0.0 107.0 %moe_block.1 = bf16[128,2048]{1,0:T(8,128)(2,1)} custom-call(bf16[128,2048]{1,0:T(8,128)(2,1)} %x_ref.1, s32[8,128]{1,0:T(8,128)} %bitcast.3, bf16[2048]{0:T(1024)(128)(2,1)} %gain_ref.1, bf16[64,2048]{1,0:T(8,128)(2,1)} %bitcast.2, bf16[8,2048,1024]{2,1,0:T(8,128)(2,1)} %w1_ref.1, bf16[8,2048,1024]{2,1,0:T(8,128)(2,1)} %w3_ref.1, bf16[8,1024,2048]{2,1,0:T(8,128)(2,1)} %w2_ref.1), custom_call_target="tpu_custom_call" | custom-call | tf_op jit(solution)/shard_map/moe_block/pallas_call | solution.py:370
  107.0 1.9 %copy.9 = bf16[128,2048]{1,0:T(8,128)(2,1)} copy(bf16[128,2048]{1,0:T(8,128)(2,1)} %moe_block.1) | data formatting | bytes 1048576

commit v3 on v2

--- a/solution.py
+++ b/solution.py
@@ -12,14 +12,15 @@
 F32, BF16, I32 = jnp.float32, jnp.bfloat16, jnp.int32
 FC = 128
 CC = 256
+NSLOT = 3
 NQ = 4
 WIN = 256
 RG = 16
 
 
-def moe_kernel(dims, x_ref, ids_ref, gain_ref, wr_ref, w1_ref, w3_ref, w2_ref, out_ref,
-               xg, idsg, gsrc, gdst, gbuf, xs, hbuf, pbuf, gates, wa, wb, obuf, part, rd, rp1, rp2,
-               meta_v, meta_s, posrow,
+def moe_kernel(dims, x_hbm, ids_hbm, gain_hbm, wr_hbm, w1_ref, w3_ref, w2_ref, out_ref,
+               x_ref, gain_ref, wr_ref, xg, idsg, gsrc, gdst, gbuf, xs, hbuf, gates, wa, wb, wc, obuf, part, rd, rp1, rp2,
+               meta_v, meta_s, posrow, posv, s_in,
                s_ids, r_ids, s_gt, r_gt, s_sib, r_sib, s_nb, r_nb, s_dg, r_dg, s_sf, r_sf, s_sd, r_sd, s_w, s_meta,
                d_s, d_r, p1_s, p1_r, p2_s, p2_r):
     T, D, FF, E, NDEV, NB = dims
@@ -37,7 +38,7 @@
         return pltpu.make_async_remote_copy(src_ref=src, dst_ref=dst, send_sem=ss, recv_sem=rs,
                                             device_id={'ep': dev}, device_id_type=MESH)
 
-    wslots = (wa, wb)
+    wslots = (wa, wb, wc)
 
     def a_copies(f, slot):
         cols = pl.ds(pl.multiple_of(f * FC, FC), FC)
@@ -49,28 +50,33 @@
         rows = pl.ds(pl.multiple_of(half * FF, FF), FF)
         return pltpu.make_async_copy(w2_ref.at[:, :, cols], wslots[slot].at[:, rows, :], s_w.at[slot, half])
 
-    for slot in range(2):
+    barrier = pltpu.get_barrier_semaphore()
+    for k in range(1, NDEV):
+        pl.semaphore_signal(barrier, inc=1, device_id={'ep': (me + k) % NDEV}, device_id_type=MESH)
+
+    ins = [pltpu.make_async_copy(a, b, s_in.at[k]) for k, (a, b) in enumerate(
+        ((x_hbm, x_ref), (gain_hbm, gain_ref), (ids_hbm, idsg.at[me]), (wr_hbm, wr_ref)))]
+    for cp in ins:
+        cp.start()
+    for slot in range(NSLOT):
         for cp in a_copies(slot, slot):
             cp.start()
 
-    barrier = pltpu.get_barrier_semaphore()
-    for k in range(1, NDEV):
-        pl.semaphore_signal(barrier, inc=1, device_id={'ep': (me + k) % NDEV}, device_id_type=MESH)
-
     own = xg.at[me // 2, core]
 
-    def norm_rows(i, carry):
-        rows = pl.ds(pl.multiple_of(i * 16, 16), 16)
+    ins[0].wait()
+    ins[1].wait()
+    gain = gain_ref[...].astype(F32).reshape(1, D)
+    for i in range(T // 16):
+        rows = pl.ds(i * 16, 16)
         t = x_ref[rows, :].astype(F32)
         inv = lax.rsqrt(jnp.mean(t * t, axis=1, keepdims=True) + NORM_EPS)
-        xg[me // 2, core, rows, :] = (t * inv * gain_ref[...].astype(F32).reshape(1, D)).astype(BF16)
-        return carry
-
-    lax.fori_loop(0, T // 16, norm_rows, 0)
+        xg[me // 2, core, rows, :] = (t * inv * gain).astype(BF16)
+    ins[2].wait()
     pl.semaphore_wait(barrier, NDEV - 1)
 
     def ids_copy(k):
-        return remote(ids_ref, idsg.at[me], s_ids.at[k - 1], r_ids.at[k - 1], (me + k) % NDEV)
+        return remote(idsg.at[me], idsg.at[me], s_ids.at[k - 1], r_ids.at[k - 1], (me + k) % NDEV)
 
     def gate_copy(k):
         to = (me + k) % NDEV
@@ -112,6 +118,7 @@
         to_nb(1, q).start()
         to_sib(q).start()
 
+    ins[3].wait()
     logits = lax.dot_general(wr_ref[...], own[...], (((1,), (1,)), ((), ())), preferred_element_type=F32)
     ex = jnp.exp(logits - jnp.max(logits, axis=0, keepdims=True))
     prob = ex / jnp.sum(ex, axis=0, keepdims=True)
@@ -119,7 +126,6 @@
         gsrc[r] = prob[r * E:(r + 1) * E]
     gdst[me] = gsrc[me]
 
-    idsg[me] = ids_ref[...]
     for k in range(1, NDEV):
         ids_copy(k).wait_recv()
     sub_e = lax.broadcasted_iota(I32, (E, T), 0)
@@ -145,11 +151,10 @@
     eid = jnp.minimum(eid, E - 1)
     base = start * T
     wst = jnp.zeros((E, T), I32)
-    poss = []
     for s in range(NDEV):
         rank = jnp.dot(masks[s].astype(F32).astype(BF16), tri, preferred_element_type=F32).astype(I32)
         pos = jnp.where(masks[s] > 0, base + rank - 1, -1)
-        poss.append(pos)
+        posv[s] = pos
         for e in range(E):
             posrow[e, s] = jnp.broadcast_to(pos[e:e + 1, :], (8, T))
         w0 = jnp.minimum(base // RG, (NB * T - WIN) // RG)
@@ -200,52 +205,59 @@
             nb_sib(k, q).wait_recv()
     gather(NQ - 1, (chip_me, chip_x, chip_y), False)
 
-    wlane = lax.broadcasted_iota(I32, (T, WIN), 1)
-
-    def windows(s):
-        padded = jnp.concatenate([poss[s], jnp.zeros((T - E, T), I32)], axis=0).astype(F32)
-        col = padded.T
-        for e in range(E):
-            pc = col[:, e:e + 1].astype(I32)
-            pbuf[s, e] = (pc == wlane + meta_s[e, s] * RG).astype(F32).astype(BF16)
-        gates[s] = jnp.concatenate([gdst[s], jnp.zeros((T - E, T), F32)], axis=0).T
-
     for k in range(1, NDEV):
         gate_copy(k).wait_recv()
     for q in range(NQ):
         for k in range(2):
             to_diag(k, q).wait_recv()
             diag_sib(k, q).start()
-        windows(2 * q)
-        windows(2 * q + 1)
         for k in range(2):
             diag_sib(k, q).wait_recv()
         gather(q, (chip_d,), True)
 
-    def hidden(g, carry):
-        for slot in range(2):
-            f = g * 2 + slot
-            for cp in a_copies(f, slot):
-                cp.wait()
-            cols = pl.ds(pl.multiple_of(f * FC, FC), FC)
-            for b in range(NB):
-                e = meta_s[E, b]
-                acc = jnp.dot(xs[b * T:(b + 1) * T, :], wslots[slot][e], preferred_element_type=F32)
-                hg, hu = acc[:, :FC], acc[:, FC:]
-                hbuf[b * T:(b + 1) * T, cols] = (jax.nn.silu(hg) * hu).astype(BF16)
-
-            @pl.when(g < NF // 2 - 1)
+    wlane = lax.broadcasted_iota(I32, (T, WIN), 1)
+
+    def window_rows(s, e):
+        return pl.ds(pl.multiple_of((s % 2 * E + e) * T, T), T)
+
+    def windows(s):
+        padded = jnp.concatenate([posv[s], jnp.zeros((T - E, T), I32)], axis=0).astype(F32)
+        col = padded.T
+        for e in range(E):
+            pc = col[:, e:e + 1].astype(I32)
+            gbuf[s // 2, window_rows(s, e), :] = (pc == wlane + meta_s[e, s] * RG).astype(F32).astype(BF16)
+        gates[s] = jnp.concatenate([gdst[s], jnp.zeros((T - E, T), F32)], axis=0).T
+
+    def hidden(f, slot):
+        for cp in a_copies(f, slot):
+            cp.wait()
+        windows(f)
+        cols = pl.ds(pl.multiple_of(f * FC, FC), FC)
+        for b in range(NB):
+            e = meta_s[E, b]
+            acc = jnp.dot(xs[b * T:(b + 1) * T, :], wslots[slot][e], preferred_element_type=F32)
+            hg, hu = acc[:, :FC], acc[:, FC:]
+            hbuf[b * T:(b + 1) * T, cols] = (jax.nn.silu(hg) * hu).astype(BF16)
+
+    def hidden_three(g, carry):
+        for slot in range(NSLOT):
+            f = g * NSLOT + slot
+            hidden(f, slot)
+
+            @pl.when(f < NF - NSLOT)
             def _():
-                for cp in a_copies(f + 2, slot):
+                for cp in a_copies(f + NSLOT, slot):
                     cp.start()
-
-            @pl.when(g >= NF // 2 - 1)
-            def _():
-                for h in range(2):
-                    b_copy(slot * 2 + h, slot, h).start()
         return carry
 
-    lax.fori_loop(0, NF // 2, hidden, 0)
+    lax.fori_loop(0, NF // NSLOT, hidden_three, 0)
+    order = (2, 0)
+    for h in range(2):
+        b_copy(h, order[0], h).start()
+    hidden(NF - 2, 0)
+    for h in range(2):
+        b_copy(2 + h, order[1], h).start()
+    hidden(NF - 1, 1)
 
     def d2d(j):
         return remote(part.at[j % 4, 1 - core], rd.at[j], d_s.at[j], d_r.at[j], sib)
@@ -265,20 +277,17 @@
             for e in range(E):
                 r0 = meta_s[e, s]
                 rows = jnp.concatenate([obuf[r0 + k] for k in range(WIN // RG)], axis=0)
-                got = jnp.dot(pbuf[s, e], rows, preferred_element_type=F32)
+                got = jnp.dot(gbuf[s // 2, window_rows(s, e), :], rows, preferred_element_type=F32)
                 acc = acc + gates[s, :, e:e + 1] * got
             for h in range(2):
                 part[c % 4, to_core, h, ch // 2, ch % 2] = acc[:, h * 128:(h + 1) * 128]
 
-    def outputs(i, half, slot):
+    def outputs(half, slot):
         rows = pl.ds(pl.multiple_of(half * FF, FF), FF)
         for b in range(NB):
             e = meta_s[E, b]
             acc = jnp.dot(hbuf[b * T:(b + 1) * T, :], wslots[slot][e, rows, :], preferred_element_type=F32)
             obuf[b * (T // RG):(b + 1) * (T // RG)] = acc.astype(BF16).reshape(T // RG, RG, CC)
-        combine(i, 1 - core)
-        d2d(i).start()
-        combine(i, core)
 
     def drain(i):
         @pl.when((i >= 1) & (i < NC + 1))
@@ -318,21 +327,25 @@
                 cp.wait_send()
 
     def four(g, carry):
-        for slot in range(2):
+        for t in range(2):
+            slot = order[t]
             for h in range(2):
-                b_copy(g * 4 + slot * 2 + h, slot, h).wait()
+                b_copy(g * 4 + t * 2 + h, slot, h).wait()
 
             def two(half, inner):
-                i = g * 4 + slot * 2 + half
-                outputs(i, half, slot)
+                i = g * 4 + t * 2 + half
+                outputs(half, slot)
                 drain(i)
+                combine(i, 1 - core)
+                d2d(i).start()
+                combine(i, core)
                 return inner
             lax.fori_loop(0, 2, two, 0)
 
             @pl.when(g < NC // 4 - 1)
             def _():
                 for h in range(2):
-                    b_copy((g + 1) * 4 + slot * 2 + h, slot, h).start()
+                    b_copy((g + 1) * 4 + t * 2 + h, slot, h).start()
         return carry
 
     lax.fori_loop(0, NC // 4, four, 0)
@@ -370,9 +383,12 @@
         return pl.pallas_call(
             functools.partial(moe_kernel, dims),
             out_shape=jax.ShapeDtypeStruct((T, D), BF16),
-            in_specs=[vmem, vmem, vmem, vmem, hbm, hbm, hbm],
+            in_specs=[hbm] * 7,
             out_specs=vmem,
             scratch_shapes=[
+                pltpu.VMEM((T, D), BF16),
+                pltpu.VMEM((D,), BF16),
+                pltpu.VMEM((ndev * E, D), BF16),
                 pltpu.VMEM((ndev // 2, 2, T, D), BF16),
                 pltpu.VMEM((ndev, top, T), I32),
                 pltpu.VMEM((ndev, E, T), F32),
@@ -380,8 +396,8 @@
                 pltpu.VMEM((ndev // 2, NB * T, 2 * T), BF16),
                 pltpu.VMEM((NB * T, D), BF16),
                 pltpu.VMEM((NB * T, FF), BF16),
-                pltpu.VMEM((ndev, E, T, WIN), BF16),
                 pltpu.VMEM((ndev, T, 128), F32),
+                pltpu.VMEM((E, D, 2 * FC), BF16),
                 pltpu.VMEM((E, D, 2 * FC), BF16),
                 pltpu.VMEM((E, D, 2 * FC), BF16),
                 pltpu.VMEM((NB * T // RG, RG, CC), BF16),
@@ -392,11 +408,13 @@
                 pltpu.VMEM((2 * E, T), I32),
                 pltpu.SMEM((2 * E, T), I32),
                 pltpu.VMEM((E, ndev, 8, T), I32),
+                pltpu.VMEM((ndev, E, T), I32),
+                dma((4,)),
                 dma((ndev - 1,)), dma((ndev - 1,)),
                 dma((ndev - 1,)), dma((ndev - 1,)),
                 dma((NQ,)), dma((NQ,)), dma((2, NQ)), dma((2, NQ)),
                 dma((2, NQ)), dma((2, NQ)), dma((2, NQ)), dma((2, NQ)), dma((2, NQ)), dma((2, NQ)),
-                dma((2, 2)), dma,
+                dma((NSLOT, 2)), dma,
                 dma((NC,)), dma((NC,)), dma((NC, 2)), dma((NC, 2)), dma((NC, 2)), dma((NC, 2)),
             ],
             compiler_params=pltpu.CompilerParams(

time: 109 us -> 113 us (1.037)
  Pallas kernels: 107 us -> 111 us
    pallas_call x1, Pallas kernels: 107 us -> 111 us  [device_step(): pl.pallas_call(functools.partial(moe_kernel, dims), out_shape=jax.ShapeDt...]
where the time goes in v3:
time: 113 us
  Pallas kernels  111 us (98%)
  local copies, waits for them, and re-layouts  1.88 us (2%)
    pallas_call x1, Pallas kernels, device_step(): pl.pallas_call(functools.partial(moe_kernel, dims), out_shape=jax.ShapeDt...  111 us

profile of v3, /device:TPU:0, one launch (start us, length us, event | category | flops | bytes accessed | tf_op | source)
XLA Modules:
  0.0 113.0 jit_solution(11561731128679290983)
XLA Ops:
  0.0 111.1 %moe_block.1 = bf16[128,2048]{1,0:T(8,128)(2,1)} custom-call(bf16[128,2048]{1,0:T(8,128)(2,1)} %x_hbm.1, s32[8,128]{1,0:T(8,128)} %bitcast.3, bf16[2048]{0:T(1024)(128)(2,1)} %gain_hbm.1, bf16[64,2048]{1,0:T(8,128)(2,1)} %bitcast.2, bf16[8,2048,1024]{2,1,0:T(8,128)(2,1)} %w1_ref.1, bf16[8,2048,1024]{2,1,0:T(8,128)(2,1)} %w3_ref.1, bf16[8,1024,2048]{2,1,0:T(8,128)(2,1)} %w2_ref.1), custom_call_target="tpu_custom_call" | custom-call | tf_op jit(solution)/shard_map/moe_block/pallas_call | solution.py:383
  111.1 1.9 %copy.9 = bf16[128,2048]{1,0:T(8,128)(2,1)} copy(bf16[128,2048]{1,0:T(8,128)(2,1)} %moe_block.1) | data formatting | bytes 1048576

commit v4 on v3

--- a/solution.py
+++ b/solution.py
@@ -89,7 +89,7 @@
     QC = D // NQ
 
     def part_of(chip, q, rows=pl.ds(0, T)):
-        return xg.at[chip, core, rows, pl.ds(q * QC, QC)]
+        return xg.at[chip, core, rows, pl.ds(pl.multiple_of(q * QC, QC), QC)]
 
     def to_sib(q):
         return remote(part_of(chip_me, q), part_of(chip_me, q), s_sib.at[q], r_sib.at[q], sib)
@@ -180,40 +180,60 @@
     MR = NB * T // 4
 
     def gather(q, chips, add):
-        cols = pl.ds(q * QC, QC)
-
-        def body(i, carry):
-            rows = pl.ds(pl.multiple_of(i * MR, 16), MR)
+        cols = pl.ds(pl.multiple_of(q * QC, QC), QC)
+        for i in range(4):
+            rows = pl.ds(i * MR, MR)
             got = None
             for chip in chips:
                 one = jnp.dot(gbuf[chip, rows, :], xg[chip, :, :, cols].reshape(2 * T, QC), preferred_element_type=F32)
                 got = one if got is None else got + one
             got = got.astype(BF16)
             xs[rows, cols] = xs[rows, cols] + got if add else got
-            return carry
-        lax.fori_loop(0, 4, body, 0)
-
-    for q in range(NQ):
+
+    def forward(q):
         for k in range(2):
             to_nb(k, q).wait_recv()
             to_diag(k, q).start()
             nb_sib(k, q).start()
-        if q > 0:
-            gather(q - 1, (chip_me, chip_x, chip_y), False)
+
+    def gather_near(q):
         to_sib(q).wait_recv()
         for k in range(2):
             nb_sib(k, q).wait_recv()
-    gather(NQ - 1, (chip_me, chip_x, chip_y), False)
-
-    for k in range(1, NDEV):
-        gate_copy(k).wait_recv()
-    for q in range(NQ):
+        gather(q, (chip_me, chip_x, chip_y), False)
+
+    def forward_diag(q):
         for k in range(2):
             to_diag(k, q).wait_recv()
             diag_sib(k, q).start()
+
+    forward(0)
+
+    def near(q, carry):
+        @pl.when(q < NQ - 1)
+        def _():
+            forward(q + 1)
+
+        @pl.when(q == NQ - 1)
+        def _():
+            forward_diag(0)
+        gather_near(q)
+        return carry
+
+    lax.fori_loop(0, NQ, near, 0)
+
+    def far(q, carry):
+        @pl.when(q < NQ - 1)
+        def _():
+            forward_diag(q + 1)
         for k in range(2):
             diag_sib(k, q).wait_recv()
         gather(q, (chip_d,), True)
+        return carry
+
+    lax.fori_loop(0, NQ, far, 0)
+    for k in range(1, NDEV):
+        gate_copy(k).wait_recv()
 
     wlane = lax.broadcasted_iota(I32, (T, WIN), 1)
 
@@ -239,25 +259,29 @@
             hg, hu = acc[:, :FC], acc[:, FC:]
             hbuf[b * T:(b + 1) * T, cols] = (jax.nn.silu(hg) * hu).astype(BF16)
 
+    order = (2, 0)
+
     def hidden_three(g, carry):
         for slot in range(NSLOT):
             f = g * NSLOT + slot
-            hidden(f, slot)
+
+            @pl.when(f < NF)
+            def _():
+                hidden(f, slot)
 
             @pl.when(f < NF - NSLOT)
             def _():
                 for cp in a_copies(f + NSLOT, slot):
                     cp.start()
-        return carry
-
-    lax.fori_loop(0, NF // NSLOT, hidden_three, 0)
-    order = (2, 0)
-    for h in range(2):
-        b_copy(h, order[0], h).start()
-    hidden(NF - 2, 0)
-    for h in range(2):
-        b_copy(2 + h, order[1], h).start()
-    hidden(NF - 1, 1)
+
+            if slot in order:
+                @pl.when((f >= NF - NSLOT) & (f < NF))
+                def _():
+                    for h in range(2):
+                        b_copy(order.index(slot) * 2 + h, slot, h).start()
+        return carry
+
+    lax.fori_loop(0, (NF + NSLOT - 1) // NSLOT, hidden_three, 0)
 
     def d2d(j):
         return remote(part.at[j % 4, 1 - core], rd.at[j], d_s.at[j], d_r.at[j], sib)

time: 113 us -> 106 us (0.938)
  Pallas kernels: 111 us -> 104 us
    pallas_call x1, Pallas kernels: 111 us -> 104 us  [device_step(): pl.pallas_call(functools.partial(moe_kernel, dims), out_shape=jax.ShapeDt...]
where the time goes in v4:
time: 106 us
  Pallas kernels  104 us (98%)
  local copies, waits for them, and re-layouts  1.88 us (2%)
    pallas_call x1, Pallas kernels, device_step(): pl.pallas_call(functools.partial(moe_kernel, dims), out_shape=jax.ShapeDt...  104 us

profile of v4, /device:TPU:0, one launch (start us, length us, event | category | flops | bytes accessed | tf_op | source)
XLA Modules:
  0.0 106.2 jit_solution(8665412096336057957)
XLA Ops:
  0.0 104.3 %moe_block.1 = bf16[128,2048]{1,0:T(8,128)(2,1)} custom-call(bf16[128,2048]{1,0:T(8,128)(2,1)} %x_hbm.1, s32[8,128]{1,0:T(8,128)} %bitcast.3, bf16[2048]{0:T(1024)(128)(2,1)} %gain_hbm.1, bf16[64,2048]{1,0:T(8,128)(2,1)} %bitcast.2, bf16[8,2048,1024]{2,1,0:T(8,128)(2,1)} %w1_ref.1, bf16[8,2048,1024]{2,1,0:T(8,128)(2,1)} %w3_ref.1, bf16[8,1024,2048]{2,1,0:T(8,128)(2,1)} %w2_ref.1), custom_call_target="tpu_custom_call" | custom-call | tf_op jit(solution)/shard_map/moe_block/pallas_call | solution.py:407
  104.3 1.9 %copy.9 = bf16[128,2048]{1,0:T(8,128)(2,1)} copy(bf16[128,2048]{1,0:T(8,128)(2,1)} %moe_block.1) | data formatting | bytes 1048576

commit v5 on v4

--- a/solution.py
+++ b/solution.py
@@ -58,7 +58,7 @@
         ((x_hbm, x_ref), (gain_hbm, gain_ref), (ids_hbm, idsg.at[me]), (wr_hbm, wr_ref)))]
     for cp in ins:
         cp.start()
-    for slot in range(NSLOT):
+    def first_weights(slot):
         for cp in a_copies(slot, slot):
             cp.start()
 
@@ -208,8 +208,17 @@
             diag_sib(k, q).start()
 
     forward(0)
+    first_weights(0)
 
     def near(q, carry):
+        @pl.when(q == 1)
+        def _():
+            first_weights(1)
+
+        @pl.when(q == NQ - 1)
+        def _():
+            first_weights(2)
+
         @pl.when(q < NQ - 1)
         def _():
             forward(q + 1)
@@ -313,7 +322,7 @@
             acc = jnp.dot(hbuf[b * T:(b + 1) * T, :], wslots[slot][e, rows, :], preferred_element_type=F32)
             obuf[b * (T // RG):(b + 1) * (T // RG)] = acc.astype(BF16).reshape(T // RG, RG, CC)
 
-    def drain(i):
+    def stage_one(i):
         @pl.when((i >= 1) & (i < NC + 1))
         def _():
             j = i - 1
@@ -325,6 +334,7 @@
             for cp in first_hop(j):
                 cp.start()
 
+    def stage_two(i):
         @pl.when((i >= 2) & (i < NC + 2))
         def _():
             j = i - 2
@@ -359,10 +369,11 @@
             def two(half, inner):
                 i = g * 4 + t * 2 + half
                 outputs(half, slot)
-                drain(i)
+                stage_one(i)
                 combine(i, 1 - core)
                 d2d(i).start()
                 combine(i, core)
+                stage_two(i)
                 return inner
             lax.fori_loop(0, 2, two, 0)
 
@@ -375,7 +386,8 @@
     lax.fori_loop(0, NC // 4, four, 0)
 
     def last(i, carry):
-        drain(i)
+        stage_one(i)
+        stage_two(i)
         return carry
 
     lax.fori_loop(NC, NC + 3, last, 0)
@@ -406,7 +418,7 @@
         dma = pltpu.SemaphoreType.DMA
         return pl.pallas_call(
             functools.partial(moe_kernel, dims),
-            out_shape=jax.ShapeDtypeStruct((T, D), BF16),
+            out_shape=pltpu.VMEM((T, D), BF16),
             in_specs=[hbm] * 7,
             out_specs=vmem,
             scratch_shapes=[
@@ -442,7 +454,7 @@
                 dma((NC,)), dma((NC,)), dma((NC, 2)), dma((NC, 2)), dma((NC, 2)), dma((NC, 2)),
             ],
             compiler_params=pltpu.CompilerParams(
-                collective_id=0, has_side_effects=True, vmem_limit_bytes=67043328),
+                collective_id=0, has_side_effects=True, vmem_limit_bytes=66300000),
             name='moe_block',
         )(tokens, expert_ids.T, norm_gain, w_router.T, w_gate, w_up, w_down)
 

time: 106 us -> 97.3 us (0.918)
  Pallas kernels: 104 us -> 96.4 us
  local copies, waits for them, and re-layouts: 1.88 us -> 0.8 us
    pallas_call x1, Pallas kernels: 104 us -> 96.4 us  [device_step(): pl.pallas_call(functools.partial(moe_kernel, dims), out_shape=pltpu.VMEM(...]
    unnamed x1, local copies, waits for them, and re-layouts: 1.88 us -> 0.8 us
where the time goes in v5:
time: 97.3 us; the launch traced here: 97.2 us
  Pallas kernels  96.4 us (99%)
    pallas_call x1, Pallas kernels, device_step(): pl.pallas_call(functools.partial(moe_kernel, dims), out_shape=pltpu.VMEM(...  96.4 us

profile of v5, /device:TPU:0, one launch (start us, length us, event | category | flops | bytes accessed | tf_op | source)
XLA Modules:
  0.0 97.2 jit_solution(2973072447754937559)
XLA Ops:
  0.0 96.4 %moe_block.1 = bf16[128,2048]{1,0:T(8,128)(2,1)S(1)} custom-call(bf16[128,2048]{1,0:T(8,128)(2,1)} %x_hbm.1, s32[8,128]{1,0:T(8,128)} %bitcast.3, bf16[2048]{0:T(1024)(128)(2,1)} %gain_hbm.1, bf16[64,2048]{1,0:T(8,128)(2,1)} %bitcast.2, bf16[8,2048,1024]{2,1,0:T(8,128)(2,1)} %w1_ref.1, bf16[8,2048,1024]{2,1,0:T(8,128)(2,1)} %w3_ref.1, ...), custom_call_target="tpu_custom_call" | custom-call | tf_op jit(solution)/shard_map/moe_block/pallas_call | solution.py:419
  96.4 0.8 copy.9

commit v6 on v5

--- a/solution.py
+++ b/solution.py
@@ -372,8 +372,8 @@
                 stage_one(i)
                 combine(i, 1 - core)
                 d2d(i).start()
+                stage_two(i)
                 combine(i, core)
-                stage_two(i)
                 return inner
             lax.fori_loop(0, 2, two, 0)
 

time: 97.3 us -> 97.2 us (level)
  no operation moved by 1% of the time
where the time goes in v6:
time: 97.2 us; the launch traced here: 97.1 us
  Pallas kernels  96.3 us (99%)
    pallas_call x1, Pallas kernels, device_step(): pl.pallas_call(functools.partial(moe_kernel, dims), out_shape=pltpu.VMEM(...  96.3 us

profile of v6, /device:TPU:0, one launch (start us, length us, event | category | flops | bytes accessed | tf_op | source)
XLA Modules:
  0.0 97.1 jit_solution(9828356844665495711)
XLA Ops:
  0.0 96.3 %moe_block.1 = bf16[128,2048]{1,0:T(8,128)(2,1)S(1)} custom-call(bf16[128,2048]{1,0:T(8,128)(2,1)} %x_hbm.1, s32[8,128]{1,0:T(8,128)} %bitcast.3, bf16[2048]{0:T(1024)(128)(2,1)} %gain_hbm.1, bf16[64,2048]{1,0:T(8,128)(2,1)} %bitcast.2, bf16[8,2048,1024]{2,1,0:T(8,128)(2,1)} %w1_ref.1, bf16[8,2048,1024]{2,1,0:T(8,128)(2,1)} %w3_ref.1, ...), custom_call_target="tpu_custom_call" | custom-call | tf_op jit(solution)/shard_map/moe_block/pallas_call | solution.py:419
  96.3 0.8 copy.9
